TPU v7x, 128 devices: a whole 4x4x4 slice. The times are simulated.
128 devices in a mesh: seq: 64 (over z, x, y), feat: 2 (over core).
Axes of the slice: x: 4, y: 4, z: 4, core: 2. Of those that a mesh axis runs over, the one named last changes fastest.
Arguments:
- tokens: bfloat16 [524288, 1280], P(('seq', 'feat')), may hold values from -12 to 12
- shot_starts: int32 [128], replicated, may hold values from 0 to 521728, as said below
- seed_offsets: int32 [128, 64], replicated, may hold values from 0 to 1023, as said below
- norm_gain: float32 [1280], replicated, may hold values from 0.5 to 1.5
- proj_weight: bfloat16 [1280, 8192], P(None, 'feat'), may hold values from -0.15625 to 0.15625
Outputs:
- projected: bfloat16 [8192, 8192], P('seq', 'feat')
Inputs may be any that keep to these rules, and one draw needn't show every extreme that they name: shot_starts[0] = 0, the starts rise, and shot s starts within 1536 tokens of s * 4096, so a shot has 1024 to 7168 tokens. `seed_offsets`: each row holds 64 different offsets, all below 1024.
All inputs are finite; a program needn't handle non-finite values.
Results may differ from a plain program's by a relative error of at most 0.0055.
Values may be sent and summed in bfloat16 or wider, within the bound.
A program may use at most 128 MiB of HBM per device.

v0:
```python
import math

import jax
import jax.numpy as jnp
from jax import lax
from jax.sharding import PartitionSpec as P

ITERS = 3


def extended(x, sides, width):
    edges = {}
    for axis, dim in sides:
        size, length = (lax.axis_size(axis), x.shape[dim])
        up = [(i, (i + 1) % size) for i in range(size - 1)]
        last = lax.slice_in_dim(x, length - width, length, axis=dim)
        leading = lax.slice_in_dim(x, 0, width, axis=dim)
        edges[dim] = (
            lax.ppermute(last, axis, up),
            lax.ppermute(leading, axis, [(b, a) for a, b in up]),
        )
    done = []
    for _, dim in sides:
        low, high = edges[dim]
        around = [(width, width) if d in done else (0, 0) for d in range(x.ndim)]
        x = jnp.concatenate([jnp.pad(low, around), x, jnp.pad(high, around)], axis=dim)
        done.append(dim)
    return x


def in_order(tiles, dim):
    shape = list(tiles.shape[1:])
    shape[dim] *= tiles.shape[0]
    return jnp.moveaxis(tiles, 0, dim).reshape(shape)


def from_everyone(x, axis):
    size = lax.axis_size(axis)
    return lax.all_to_all(jnp.broadcast_to(x[None], (size, *x.shape)), axis, 0, 0, tiled=True)


def collect(x, axis, dim):
    return in_order(from_everyone(x, axis), dim)


def window_centroids(tokens, seed_offsets, shot_begin, shot_end, offset_base, device_index):
    rows_here, feature_width = tokens.shape
    rims = 3 * rows_here // 8
    window = extended(tokens, ((("seq", "feat"), 0),), rims)
    window_start = offset_base - rims
    window_place = window_start + jnp.arange(window.shape[0], dtype=jnp.int32)
    inside = ((window_place >= shot_begin[1]) & (window_place < shot_end[1])).astype(jnp.float32)
    own_seeds = lax.dynamic_slice_in_dim(seed_offsets, device_index, 1, 0)[0]
    seed_rows = shot_begin[1] + own_seeds - window_start
    own_centroid = jnp.take(window, seed_rows, axis=0).astype(jnp.float32)
    factor = 1.0 / math.sqrt(feature_width)
    for iteration in range(ITERS):
        scores = (
            lax.dot_general(
                own_centroid.astype(jnp.bfloat16),
                window,
                (((1,), (1,)), ((), ())),
                preferred_element_type=jnp.float32,
            )
            * factor
        )
        weights = jax.nn.softmax(scores, axis=0) * inside[None, :]
        own_mass = jnp.sum(weights, axis=1)
        own_sums = jnp.dot(weights.astype(jnp.bfloat16), window, preferred_element_type=jnp.float32)
        own_centroid = own_sums / own_mass[:, None]
    return own_centroid


def on_device(tokens, shot_starts, seed_offsets, norm_gain, proj_weight):
    rows_here = tokens.shape[0]
    device_count = lax.axis_size(("seq", "feat"))
    device_index = lax.axis_index(("seq", "feat"))
    offset_base = device_index * rows_here
    token_total = device_count * rows_here
    bounds = jnp.concatenate(
        [jnp.zeros((1,), jnp.int32), shot_starts, jnp.full((2,), token_total, jnp.int32)]
    )
    bounds = lax.dynamic_slice_in_dim(bounds, device_index, 4, 0)
    shot_begin = bounds[:3]
    shot_end = bounds[1:]
    own_centroid = window_centroids(
        tokens, seed_offsets, shot_begin, shot_end, offset_base, device_index
    )
    spread = jnp.sqrt(jnp.mean(own_centroid * own_centroid, axis=-1, keepdims=True) + 1e-06)
    normed = (own_centroid / spread * norm_gain).astype(jnp.bfloat16)
    projected = jnp.dot(collect(normed, "feat", 0), proj_weight, preferred_element_type=jnp.float32)
    return projected.astype(jnp.bfloat16)


def solution(mesh):
    in_specs = (P(("seq", "feat"), None), P(), P(), P(), P(None, "feat"))
    out_specs = P("seq", "feat")
    return jax.shard_map(
        on_device, mesh=mesh, in_specs=in_specs, out_specs=out_specs, check_vma=False
    )
```

profile of v0, /device:TPU:97, one launch (start us, length us, event | category | flops | bytes accessed | tf_op | source)
XLA Modules:
  0.0 151.2 jit_solution(15965551209815368708)
XLA Ops:
  0.0 5.6 %fusion.21 = (bf16[1536,1280]{1,0:T(8,128)(2,1)}, bf16[1536,1280]{1,0:T(8,128)(2,1)}) fusion(bf16[4096,1280]{1,0:T(8,128)(2,1)} %param.5), kind=kLoop, calls=%fused_computation.47 | loop fusion | bytes 15728640 | tf_op jit(solution)/shard_map/slice | solution.py:17
  5.6 3.8 %collective-permute-start = (bf16[1536,1280]{1,0:T(8,128)(2,1)}, bf16[1536,1280]{1,0:T(8,128)(2,1)}, u32[]{:S(2)}, u32[]{:S(2)}) collective-permute-start(bf16[1536,1280]{1,0:T(8,128)(2,1)} %get-tuple-element.6), channel_id=1, source_target_pairs={{0,1},{1,2},{2,3},{3,4},{4,5},{5,6},{6,7},{7,8},{8,9},{9,10},{10,1... | collective-permute-start | bytes 11796488 | tf_op jit(solution)/shard_map/ppermute | solution.py:19
  9.3 1.9 %collective-permute-start.1 = (bf16[1536,1280]{1,0:T(8,128)(2,1)}, bf16[1536,1280]{1,0:T(8,128)(2,1)}, u32[]{:S(2)}, u32[]{:S(2)}) collective-permute-start(bf16[1536,1280]{1,0:T(8,128)(2,1)} %get-tuple-element.5), channel_id=1, source_target_pairs={{1,0},{2,1},{3,2},{4,3},{5,4},{6,5},{7,6},{8,7},{9,8},{10,9},{11,1... | collective-permute-start | bytes 11796488 | tf_op jit(solution)/shard_map/ppermute | solution.py:20
  11.3 0.1 pad_add_fusion
  11.4 0.1 dynamic_slice.6
  11.4 0.6 fusion.22
  12.0 0.8 subtract_reduce_fusion
  12.9 1.3 fusion.18
  14.2 38.1 %collective-permute-done = bf16[1536,1280]{1,0:T(8,128)(2,1)} collective-permute-done((bf16[1536,1280]{1,0:T(8,128)(2,1)}, bf16[1536,1280]{1,0:T(8,128)(2,1)}, u32[]{:S(2)}, u32[]{:S(2)}) %collective-permute-start) | collective-permute-done | bytes 3932192 | tf_op jit(solution)/shard_map/ppermute | solution.py:19
  52.3 4.2 %constant_dynamic-update-slice_fusion.2 = bf16[7168,1280]{1,0:T(8,128)(2,1)} fusion(bf16[1536,1280]{1,0:T(8,128)(2,1)} %collective-permute-done), kind=kLoop, calls=%fused_computation.38 | loop fusion | bytes 7864320
  56.5 8.6 %constant_dynamic-update-slice_fusion.1 = bf16[7168,1280]{1,0:T(8,128)(2,1)} fusion(bf16[7168,1280]{1,0:T(8,128)(2,1)} %constant_dynamic-update-slice_fusion.2, bf16[4096,1280]{1,0:T(8,128)(2,1)} %param.5), kind=kLoop, calls=%fused_computation.37 | loop fusion | bytes 20971520
  65.1 0.0 collective-permute-done.1
  65.1 4.2 %constant_dynamic-update-slice_fusion = bf16[7168,1280]{1,0:T(8,128)(2,1)} fusion(bf16[7168,1280]{1,0:T(8,128)(2,1)} %constant_dynamic-update-slice_fusion.1, bf16[1536,1280]{1,0:T(8,128)(2,1)} %collective-permute-done.1), kind=kLoop, calls=%fused_computation.36 | loop fusion | bytes 7864320 | tf_op jit(solution)/shard_map/concatenate | solution.py:26
  69.3 9.4 %gather_fusion = bf16[64,1280]{1,0:T(8,128)(2,1)S(1)} fusion(bf16[7168,1280]{1,0:T(8,128)(2,1)} %constant_dynamic-update-slice_fusion, s32[1024]{0:T(1024)S(1)} %pad_clamp_fusion), kind=kCustom, calls=%fused_computation | custom fusion | bytes 327936 | tf_op jit(solution)/shard_map/jit(_take)/gather | solution.py:55
  78.8 11.9 %fusion.23 = (f32[7168]{0:T(1024)S(1)}, f32[64,7168]{1,0:T(8,128)S(1)}) fusion(bf16[7168,1280]{1,0:T(8,128)(2,1)} %constant_dynamic-update-slice_fusion, bf16[64,1280]{1,0:T(8,128)(2,1)S(1)} %gather_fusion, pred[64]{0:T(512)(128)(4,1)S(1)} %compare_and_fusion), kind=kOutput, calls=%fused_computation.49 | convolution fusion | flops 1175397376 | bytes 20377664 | tf_op jit(solution)/shard_map/dot_general | solution.py:59
  90.6 0.3 fusion.2
  90.9 0.5 fusion.9
  91.4 17.8 %fusion.24 = (f32[7168]{0:T(1024)S(1)}, f32[64,7168]{1,0:T(8,128)}) fusion(bf16[7168,1280]{1,0:T(8,128)(2,1)} %constant_dynamic-update-slice_fusion, f32[64,7168]{1,0:T(8,128)S(1)} %get-tuple-element.10, f32[7168]{0:T(1024)S(1)} %fusion.18, f32[7168]{0:T(1024)S(1)} %fusion.2, f32[7168]{0:T(1024)S(1)} %get-tuple-element.9, f32[64]{0:T(128)S(1)} %fusion.9), kind=kOutput, calls=%fused_computation.50 | convolution fusion | flops 2351719424 | bytes 22135040 | tf_op jit(solution)/shard_map/dot_general | solution.py:59
  109.2 1.9 %fusion.3 = f32[7168]{0:T(1024)S(1)} fusion(f32[64,7168]{1,0:T(8,128)} %get-tuple-element.12, f32[7168]{0:T(1024)S(1)} %get-tuple-element.11), kind=kLoop, calls=%fused_computation.16 | loop fusion | flops 910336 | bytes 1892352 | tf_op jit(solution)/shard_map/reduce_sum | solution.py:67
  111.1 0.1 copy-done
  111.3 0.5 fusion.10
  111.7 16.8 %fusion.25 = (f32[7168]{0:T(1024)S(1)}, f32[64,7168]{1,0:T(8,128)S(1)}) fusion(bf16[7168,1280]{1,0:T(8,128)(2,1)} %constant_dynamic-update-slice_fusion, f32[64,7168]{1,0:T(8,128)} %get-tuple-element.12, f32[7168]{0:T(1024)S(1)} %fusion.3, f32[7168]{0:T(1024)S(1)} %get-tuple-element.11, f32[7168]{0:T(1024)S(1)} %fusion.18, f32[64]{0:T(128)S(1)} %fusion.10), kind=kOutput, calls=%fused_computation.51 | convolution fusion | flops 2351719424 | bytes 22135040 | tf_op jit(solution)/shard_map/dot_general | solution.py:59
  128.6 0.3 fusion.4
  128.9 0.0 slice-start
  128.9 0.5 fusion.11
  129.4 0.0 copy-start.2
  129.4 0.0 slice-start.1
  129.4 0.0 slice-start.2
  129.4 9.9 %multiply_reduce_fusion = (f32[64]{0:T(128)S(1)}, f32[64,1280]{1,0:T(8,128)S(1)}) fusion(f32[64]{0:T(128)S(1)} %fusion.11, bf16[7168,1280]{1,0:T(8,128)(2,1)} %constant_dynamic-update-slice_fusion, f32[7168]{0:T(1024)S(1)} %fusion.18, f32[7168]{0:T(1024)S(1)} %fusion.4, f32[64,7168]{1,0:T(8,128)S(1)} %get-tuple-element.14, f32[7168]{0:T(1024)S(1)} %get-tuple-element.13), kind=kOutput, calls=%fused_computation.26 | convolution fusion | flops 1176485888 | bytes 20599296 | tf_op jit(solution)/shard_map/dot_general | solution.py:69
  139.4 0.1 multiply_convert_fusion
  139.5 9.2 %all_to_all.5 = bf16[2,64,1280]{2,1,0:T(8,128)(2,1)S(1)} all-to-all(bf16[2,64,1280]{2,1,0:T(8,128)(2,1)S(1)} %broadcast_in_dim.14), channel_id=1, replica_groups=mesh['seq'=64,'feat'=2] {'feat'}, dimensions={0} | all-to-all | bytes 655360 | tf_op jit(solution)/shard_map/all_to_all | solution.py:39
  148.7 2.5 %convolution_convert_fusion = bf16[128,4096]{1,0:T(8,128)(2,1)} fusion(bf16[128,1280]{1,0:T(8,128)(2,1)S(1)} %bitcast.27, bf16[1280,4096]{1,0:T(8,128)(2,1)S(1)} %bitcast.26), kind=kOutput, calls=%fused_computation.4 | convolution fusion | flops 1342701568 | bytes 11862016 | tf_op jit(solution)/shard_map/dot_general | solution.py:91
  (16 shorter events, 0.1 us)
Async XLA Ops:
  0.0 11.3 %copy-start.3 = (s32[128]{0:T(128)S(1)}, s32[128]{0:T(128)}, u32[]{:S(2)}) copy-start(s32[128]{0:T(128)} %param.6) | copy-start | bytes 1540
  0.0 12.0 %copy-start.1 = (s32[128,64]{0,1:T(8,128)S(1)}, s32[128,64]{0,1:T(8,128)}, u32[]{:S(2)}) copy-start(s32[128,64]{0,1:T(8,128)} %param.7) | copy-start | bytes 98308
  5.6 46.7 %collective-permute-start = (bf16[1536,1280]{1,0:T(8,128)(2,1)}, bf16[1536,1280]{1,0:T(8,128)(2,1)}, u32[]{:S(2)}, u32[]{:S(2)}) collective-permute-start(bf16[1536,1280]{1,0:T(8,128)(2,1)} %get-tuple-element.6), channel_id=1, source_target_pairs={{0,1},{1,2},{2,3},{3,4},{4,5},{5,6},{6,7},{7,8},{8,9},{9,10},{10,1... | collective-permute-start | bytes 11796488 | tf_op jit(solution)/shard_map/ppermute | solution.py:19
  9.3 55.8 %collective-permute-start.1 = (bf16[1536,1280]{1,0:T(8,128)(2,1)}, bf16[1536,1280]{1,0:T(8,128)(2,1)}, u32[]{:S(2)}, u32[]{:S(2)}) collective-permute-start(bf16[1536,1280]{1,0:T(8,128)(2,1)} %get-tuple-element.5), channel_id=1, source_target_pairs={{1,0},{2,1},{3,2},{4,3},{5,4},{6,5},{7,6},{8,7},{9,8},{10,9},{11,1... | collective-permute-start | bytes 11796488 | tf_op jit(solution)/shard_map/ppermute | solution.py:20
  109.2 2.1 %copy-start = (f32[64,7168]{1,0:T(8,128)S(1)}, f32[64,7168]{1,0:T(8,128)}, u32[]{:S(2)}) copy-start(f32[64,7168]{1,0:T(8,128)} %get-tuple-element.12) | copy-start | bytes 5505028
  128.9 19.8 %slice-start = ((s8[10485760]{0:T(1024)(128)(4,1)}), s8[4194304]{0:T(1024)(128)(4,1)S(1)}, s32[]{:S(2)}) async-start(s8[10485760]{0:T(1024)(128)(4,1)} %bitcast.25), calls=%async_computation.1 | async-start | bytes 8388608
  129.4 10.0 %copy-start.2 = (f32[1280]{0:T(1024)S(1)}, f32[1280]{0:T(1024)}, u32[]{:S(2)}) copy-start(f32[1280]{0:T(1024)} %param.8) | copy-start | bytes 15364
  129.4 19.3 %slice-start.1 = ((s8[10485760]{0:T(1024)(128)(4,1)}), s8[4194304]{0:T(1024)(128)(4,1)S(1)}, s32[]{:S(2)}) async-start(s8[10485760]{0:T(1024)(128)(4,1)} %bitcast.25), calls=%async_computation.2 | async-start | bytes 8388608
  129.4 19.3 %slice-start.2 = ((s8[10485760]{0:T(1024)(128)(4,1)}), s8[2097152]{0:T(1024)(128)(4,1)S(1)}, s32[]{:S(2)}) async-start(s8[10485760]{0:T(1024)(128)(4,1)} %bitcast.25), calls=%async_computation.3 | async-start | bytes 4194304
where the time goes:
time: 152 us; the launch traced here: 151 us
  matrix products  59 us (39%)
  waiting for transfers between devices  38.1 us (25%)
  local copies, waits for them, and re-layouts  32.9 us (22%)
  blocking collectives  9.15 us (6%)
  other arithmetic  6.26 us (4%)
  starting transfers between devices  5.68 us (4%)
    dot_general x3, matrix products, window_centroids(): lax.dot_general(own_centroid.astype(jnp.bfloat16), window, (((1,), (1,)),...  46.5 us
    ppermute x1, waiting for transfers between devices, extended(): lax.ppermute(last, axis, up)  38.1 us
    unnamed x16, local copies, waits for them, and re-layouts  13 us
    dot_general x1, matrix products, window_centroids(): jnp.dot(weights.astype(jnp.bfloat16), window, preferred_element_type=jnp....  9.93 us
    gather x1, local copies, waits for them, and re-layouts, window_centroids(): own_centroid = jnp.take(window, seed_rows, axis=0).astype(jnp.float32)  9.42 us
    all_to_all x1, blocking collectives, from_everyone(): lax.all_to_all(jnp.broadcast_to(x[None], (size, *x.shape)), axis, 0, 0, t...  9.15 us
    slice x1, local copies, waits for them, and re-layouts, extended(): leading = lax.slice_in_dim(x, 0, width, axis=dim)  5.55 us
    concatenate x1, local copies, waits for them, and re-layouts, extended(): jnp.concatenate([jnp.pad(low, around), x, jnp.pad(high, around)], axis=dim)  4.23 us
  transfers between devices with their start and end apart: 2, of which 1 were waited for; matrix products, arithmetic and copies ran while one was open for 10% of the time, Pallas kernels for 0%

commit v1 on v0

v1 whole, which is shorter than its diff:
```python
import functools
import math

import jax
import jax.numpy as jnp
from jax import lax
from jax.experimental import pallas as pl
from jax.experimental.pallas import tpu as pltpu
from jax.sharding import PartitionSpec as P

MESH = pl.DeviceIdType.MESH
ITERS = 3
ROUNDS = ITERS + 1
K = 64
CHUNK = 256
TILE = 256
COLS = 512


def kernel(
    seq_size,
    starts,
    seeds,
    gain,
    tok_hbm,
    w_hbm,
    out_hbm,
    x,
    wp,
    outs,
    s,
    wt,
    c,
    po,
    px,
    pnb,
    si,
    qo,
    tb,
    ub,
    co,
    ci,
    mn,
    mo,
    mi,
    mq,
    mt,
    mu,
    rec,
    cent,
    ns,
    nm,
    x_sem,
    w_sem,
    o_sem,
    p_send,
    p_recv,
    t_send,
    t_recv,
    c_send,
    c_recv,
    mp_send,
    mp_recv,
    mt_send,
    mt_recv,
    n_send,
    n_recv,
):
    chunks, rows, _ = x.shape
    half = rows // 2
    tiles = half // TILE
    col_tiles = wp.shape[0]
    width = chunks * CHUNK
    f32, bf16 = jnp.float32, jnp.bfloat16

    seq = lax.axis_index("seq")
    feat = lax.axis_index("feat")
    me = seq * 2 + feat
    count = seq_size * 2
    inner = (seq, 1 - feat)
    outer_seq = seq + 2 * feat - 1
    has_outer = jnp.logical_and(outer_seq >= 0, outer_seq < seq_size)
    outer = (outer_seq, 1 - feat)
    h_in, h_out = 1 - feat, feat

    def token_copy(f):
        return pltpu.make_async_copy(
            tok_hbm.at[:, pl.ds(pl.multiple_of(f * CHUNK, CHUNK), CHUNK)], x.at[f], x_sem.at[f]
        )

    def weight_copy(n):
        return pltpu.make_async_copy(
            w_hbm.at[:, pl.ds(pl.multiple_of(n * COLS, COLS), COLS)], wp.at[n], w_sem.at[n]
        )

    def out_copy(n):
        return pltpu.make_async_copy(
            outs.at[n], out_hbm.at[:, pl.ds(pl.multiple_of(n * COLS, COLS), COLS)], o_sem.at[n]
        )

    def remote(src, dst, send, recv, device):
        return pltpu.make_async_remote_copy(
            src_ref=src,
            dst_ref=dst,
            send_sem=send,
            recv_sem=recv,
            device_id=device,
            device_id_type=MESH,
        )

    def p_copy(r, f):
        return remote(si.at[r, f], qo.at[r, f], p_send.at[r, f], p_recv.at[r, f], inner)

    def t_copy(r, f):
        return remote(tb.at[r, f], ub.at[r, f], t_send.at[r, f], t_recv.at[r, f], outer)

    def c_copy(r, f):
        return remote(co.at[r, f], ci.at[r, f], c_send.at[r, f], c_recv.at[r, f], inner)

    def mp_copy(r):
        return remote(mi.at[r], mq.at[r], mp_send.at[r], mp_recv.at[r], inner)

    def mt_copy(r):
        return remote(mt.at[r], mu.at[r], mt_send.at[r], mt_recv.at[r], outer)

    def n_copy():
        return remote(ns, nm.at[pl.ds(feat * K, K)], n_send, n_recv, inner)

    @pl.loop(0, chunks)
    def _(f):
        token_copy(f).start()

    barrier = pltpu.get_barrier_semaphore()
    pl.semaphore_signal(barrier, inc=1, device_id=inner, device_id_type=MESH)

    @pl.when(has_outer)
    def _():
        pl.semaphore_signal(barrier, inc=1, device_id=outer, device_id_type=MESH)

    base = me * rows
    start = starts[me] - base
    following = starts[jnp.minimum(me + 1, count - 1)]
    end = jnp.where(me == count - 1, count * rows, following) - base

    def is_mine(shape):
        first = jnp.full(shape, start, jnp.int32) < 0
        last = jnp.full(shape, end, jnp.int32) >= rows
        left = jnp.full(shape, feat, jnp.int32) == 0
        return jnp.logical_or(
            jnp.logical_and(left, first), jnp.logical_and(jnp.logical_not(left), last)
        )

    @pl.when(jnp.logical_not(has_outer))
    def _():
        ub[...] = jnp.zeros_like(ub)
        mu[...] = jnp.zeros_like(mu)

    def column(row, offset):
        spread = jnp.broadcast_to(seeds[pl.ds(row, 1), :].astype(f32), (K, K))
        return spread.T[:, :1].astype(jnp.int32) + offset

    own_at = column(me, start)
    next_at = column(jnp.minimum(me + 1, count - 1), end)

    def lanes(h, t):
        return lax.broadcasted_iota(jnp.int32, (K, TILE), 1) + (h * half + t * TILE)

    def place(t):
        return pl.ds(pl.multiple_of(t * TILE, TILE), TILE)

    def fold(w):
        total = w[:, :128]
        for i in range(1, TILE // 128):
            total = total + w[:, i * 128 : (i + 1) * 128]
        return total

    def put(h, t, nb, own):
        wt[h, :K, place(t)] = nb.astype(bf16)
        wt[h, K:, place(t)] = own.astype(bf16)

    zero = jnp.zeros((K, 128), f32)

    def note_mass(r, nbs, own):
        def total(m):
            return jnp.broadcast_to(jnp.sum(m, axis=1, keepdims=True), (K, 128))

        mn[0] = total(nbs[0])
        mn[1] = total(nbs[1])
        mo[...] = total(own)
        mi[r] = mn[h_in]
        mp_copy(r).start()

    nbs, own_mass = [], zero
    for h in range(2):

        def seed_tile(t, carry, h=h):
            nb_mass, own_mass = carry
            at = lanes(h, t)
            own = (at == own_at).astype(f32)
            nb = (at == next_at).astype(f32) if h else jnp.zeros((K, TILE), f32)
            put(h, t, nb, own)
            return nb_mass + fold(nb), own_mass + fold(own)

        nb_mass, own_mass = lax.fori_loop(0, tiles, seed_tile, (zero, own_mass))
        nbs.append(nb_mass)

    pl.semaphore_wait(barrier, 1 + has_outer.astype(jnp.int32))

    note_mass(0, nbs, own_mass)

    def wide(m):
        return jnp.concatenate([m] * (CHUNK // 128), axis=1)

    def round_body(r, carry):
        def sums(f):
            @pl.when(r == 0)
            def _():
                token_copy(f).wait()

            low = jnp.dot(wt[0], x[f, :half], preferred_element_type=f32)
            high = jnp.dot(wt[1], x[f, half:], preferred_element_type=f32)
            pnb[0] = low[:K]
            pnb[1] = high[:K]
            po[f] = low[K:] + high[K:]
            px[f] = pnb[h_out]
            si[r, f] = pnb[h_in]
            p_copy(r, f).start()

        def pass_on(f):
            p_copy(r, f).wait_recv()
            chip = po[f] + qo[r, f]
            po[f] = chip
            tb[r, f] = jnp.where(is_mine((K, CHUNK)), chip, px[f]).astype(bf16)

            @pl.when(has_outer)
            def _():
                t_copy(r, f).start()

        def pass_mass_on():
            mp_copy(r).wait_recv()
            chip = mo[...] + mq[r]
            mo[...] = chip
            mt[r] = jnp.where(is_mine((K, 128)), chip, mn[h_out])

            @pl.when(has_outer)
            def _():
                mt_copy(r).start()

        @pl.loop(0, chunks + 2)
        def _(f):
            @pl.when(f < chunks)
            def _():
                sums(f)

            @pl.when(f == 2)
            def _():
                pass_mass_on()

            @pl.when(f >= 2)
            def _():
                pass_on(f - 2)

        @pl.when(r == 0)
        def _():
            @pl.loop(0, col_tiles)
            def _(n):
                weight_copy(n).start()

        s[...] = jnp.zeros_like(s)

        @pl.when(has_outer)
        def _():
            mt_copy(r).wait_recv()

        mine = is_mine((K, 128))
        m_own = mo[...] + jnp.where(mine, mu[r], 0.0)
        m_nb = mn[h_out] + jnp.where(mine, 0.0, mu[r])
        rec[0] = 1.0 / m_own
        rec[1] = 1.0 / jnp.where(m_nb > 0.0, m_nb, 1.0)

        def arrive(f):
            @pl.when(has_outer)
            def _():
                t_copy(r, f).wait_recv()

            mine = is_mine((K, CHUNK))
            u = ub[r, f].astype(f32)
            own = (po[f] + jnp.where(mine, u, 0.0)) * wide(rec[0])
            cent[f] = own
            return (px[f] + jnp.where(mine, 0.0, u)) * wide(rec[1])

        def spread(f):
            nb = arrive(f)
            own = cent[f].astype(bf16)
            co[r, f] = own
            c_copy(r, f).start()
            c[0, f, K:] = own
            c[1, f, K:] = own
            c[h_out, f, :K] = nb.astype(bf16)

        def score(f):
            c_copy(r, f).wait_recv()
            c[h_in, f, :K] = ci[r, f]
            for h in range(2):
                s[h * half : (h + 1) * half] += lax.dot_general(
                    x[f, h * half : (h + 1) * half],
                    c[h, f],
                    (((1,), (1,)), ((), ())),
                    preferred_element_type=f32,
                )

        def soften():
            scale = math.log2(math.e) / math.sqrt(width)
            nbs, own_mass = [], zero
            for h in range(2):

                def tile(t, carry, h=h):
                    nb_mass, own_mass = carry
                    at = pl.ds(pl.multiple_of(h * half + t * TILE, TILE), TILE)
                    flat = s[at].T
                    where = lanes(h, t)
                    is_nb = (where >= end) if h else (where < start)
                    mixed = jnp.where(is_nb, flat[:K], flat[K:])
                    e = jnp.exp2((mixed - jnp.max(mixed, axis=0, keepdims=True)) * scale)
                    w = e * (1.0 / jnp.sum(e, axis=0, keepdims=True))
                    nb = jnp.where(is_nb, w, 0.0)
                    own = jnp.where(is_nb, 0.0, w)
                    put(h, t, nb, own)
                    return nb_mass + fold(nb), own_mass + fold(own)

                nb_mass, own_mass = lax.fori_loop(0, tiles, tile, (zero, own_mass))
                nbs.append(nb_mass)
            note_mass(r + 1, nbs, own_mass)

        @pl.when(r < ITERS)
        def _():
            @pl.loop(0, chunks + 2)
            def _(f):
                @pl.when(f < chunks)
                def _():
                    spread(f)

                @pl.when(f >= 2)
                def _():
                    score(f - 2)

            soften()

        @pl.when(r == ITERS)
        def _():
            @pl.loop(0, chunks)
            def _(f):
                arrive(f)

        return carry

    lax.fori_loop(0, ROUNDS, round_body, 0)

    square = jnp.zeros((K, 1), f32)
    for f in range(chunks):
        square = square + jnp.sum(cent[f] * cent[f], axis=1, keepdims=True)
    inverse = 1.0 / jnp.sqrt(square / width + 1e-06)
    for f in range(chunks):
        at = slice(f * CHUNK, (f + 1) * CHUNK)
        normed = (cent[f] * inverse * gain[:, at]).astype(bf16)
        ns[:, at] = normed
        nm[pl.ds(pl.multiple_of(feat * K, K), K), at] = normed
    n_copy().start()
    n_copy().wait_recv()

    @pl.loop(0, col_tiles)
    def _(n):
        weight_copy(n).wait()
        outs[n] = jnp.dot(nm[...], wp[n], preferred_element_type=f32).astype(bf16)
        out_copy(n).start()

    n_copy().wait_send()

    @pl.loop(0, ROUNDS)
    def _(r):
        mp_copy(r).wait_send()

        @pl.when(has_outer)
        def _():
            mt_copy(r).wait_send()

        @pl.loop(0, chunks)
        def _(f):
            p_copy(r, f).wait_send()

            @pl.when(r < ITERS)
            def _():
                c_copy(r, f).wait_send()

            @pl.when(has_outer)
            def _():
                t_copy(r, f).wait_send()

    @pl.loop(0, col_tiles)
    def _(n):
        out_copy(n).wait()


def on_device(seq_size, tokens, shot_starts, seed_offsets, norm_gain, proj_weight):
    rows, width = tokens.shape
    columns = proj_weight.shape[1]
    chunks = width // CHUNK
    col_tiles = columns // COLS
    half = rows // 2
    f32, bf16 = jnp.float32, jnp.bfloat16
    vmem, dma = pltpu.VMEM, pltpu.SemaphoreType.DMA
    piece = (K, CHUNK)
    return pl.pallas_call(
        functools.partial(kernel, seq_size),
        out_shape=jax.ShapeDtypeStruct((2 * K, columns), bf16),
        in_specs=[
            pl.BlockSpec(memory_space=pltpu.SMEM),
            pl.BlockSpec(memory_space=pltpu.VMEM),
            pl.BlockSpec(memory_space=pltpu.VMEM),
            pl.BlockSpec(memory_space=pl.ANY),
            pl.BlockSpec(memory_space=pl.ANY),
        ],
        out_specs=pl.BlockSpec(memory_space=pl.ANY),
        scratch_shapes=[
            vmem((chunks, rows, CHUNK), bf16),
            vmem((col_tiles, width, COLS), bf16),
            vmem((col_tiles, 2 * K, COLS), bf16),
            vmem((rows, 2 * K), f32),
            vmem((2, 2 * K, half), bf16),
            vmem((2, chunks, 2 * K, CHUNK), bf16),
            vmem((chunks, *piece), f32),
            vmem((chunks, *piece), f32),
            vmem((2, *piece), f32),
            vmem((ROUNDS, chunks, *piece), f32),
            vmem((ROUNDS, chunks, *piece), f32),
            vmem((ROUNDS, chunks, *piece), bf16),
            vmem((ROUNDS, chunks, *piece), bf16),
            vmem((ITERS, chunks, *piece), bf16),
            vmem((ITERS, chunks, *piece), bf16),
            vmem((2, K, 128), f32),
            vmem((K, 128), f32),
            vmem((ROUNDS, K, 128), f32),
            vmem((ROUNDS, K, 128), f32),
            vmem((ROUNDS, K, 128), f32),
            vmem((ROUNDS, K, 128), f32),
            vmem((2, K, 128), f32),
            vmem((chunks, *piece), f32),
            vmem((K, width), bf16),
            vmem((2 * K, width), bf16),
            dma((chunks,)),
            dma((col_tiles,)),
            dma((col_tiles,)),
            dma((ROUNDS, chunks)),
            dma((ROUNDS, chunks)),
            dma((ROUNDS, chunks)),
            dma((ROUNDS, chunks)),
            dma((ITERS, chunks)),
            dma((ITERS, chunks)),
            dma((ROUNDS,)),
            dma((ROUNDS,)),
            dma((ROUNDS,)),
            dma((ROUNDS,)),
            dma,
            dma,
        ],
        compiler_params=pltpu.CompilerParams(
            collective_id=0, has_side_effects=True, vmem_limit_bytes=60 * 2**20
        ),
    )(shot_starts, seed_offsets, norm_gain[None, :], tokens, proj_weight)


def solution(mesh):
    in_specs = (P(("seq", "feat"), None), P(), P(), P(), P(None, "feat"))
    out_specs = P("seq", "feat")
    return jax.shard_map(
        functools.partial(on_device, mesh.shape["seq"]),
        mesh=mesh,
        in_specs=in_specs,
        out_specs=out_specs,
        check_vma=False,
    )
```

time: 152 us -> 65.8 us (0.43)
  Pallas kernels: 0 us -> 60.5 us
  matrix products: 59 us -> 0 us
  waiting for transfers between devices: 38.1 us -> 0 us
  local copies, waits for them, and re-layouts: 32.9 us -> 5.06 us
  blocking collectives: 9.15 us -> 0 us
  other arithmetic: 6.26 us -> 0 us
  starting transfers between devices: 5.68 us -> 0 us
    pallas_call x0 -> x1, Pallas kernels: none -> 60.5 us  [on_device(): pl.pallas_call(functools.partial(kernel, seq_size), out_shape=jax.ShapeDt...]
    dot_general x5 -> x0, matrix products: 59 us -> none  [the longest x3 46.5 us: window_centroids(): lax.dot_general(own_centroid.astype(jnp.bfloat16), window, (((1,), (1,)),...]
    ppermute x2 -> x0, waiting for transfers between devices: 38.1 us -> none  [the longest x1 38.1 us: extended(): lax.ppermute(last, axis, up)]
    gather x1 -> x0, local copies, waits for them, and re-layouts: 9.42 us -> none  [window_centroids(): own_centroid = jnp.take(window, seed_rows, axis=0).astype(jnp.float32)]
    unnamed x16 -> x2, local copies, waits for them, and re-layouts: 13 us -> 3.77 us
    all_to_all x1 -> x0, blocking collectives: 9.15 us -> none  [from_everyone(): lax.all_to_all(jnp.broadcast_to(x[None], (size, *x.shape)), axis, 0, 0, t...]
    slice x2 -> x0, local copies, waits for them, and re-layouts: 6.17 us -> none  [the longest x1 5.55 us: extended(): leading = lax.slice_in_dim(x, 0, width, axis=dim)]
    ppermute x2 -> x0, starting transfers between devices: 5.68 us -> none  [the longest x1 3.75 us: extended(): lax.ppermute(last, axis, up)]
  transfers between devices with their start and end apart: 2 -> 0, of which waited for: 1 -> 0; matrix products, arithmetic and copies ran while one was open for 10% -> 0% of each run, Pallas kernels for 0% -> 0%
where the time goes in v1:
time: 65.8 us; the launch traced here: 65.5 us
  Pallas kernels  60.5 us (92%)
  local copies, waits for them, and re-layouts  5.06 us (8%)
    pallas_call x1, Pallas kernels, on_device(): pl.pallas_call(functools.partial(kernel, seq_size), out_shape=jax.ShapeDt...  60.5 us
    unnamed x2, local copies, waits for them, and re-layouts  3.77 us

profile of v1, /device:TPU:97, one launch (start us, length us, event | category | flops | bytes accessed | tf_op | source)
XLA Modules:
  0.0 65.5 jit_solution(2677345871912134411)
XLA Ops:
  0.0 1.3 %broadcast_in_dim.3.gain = f32[1,1280]{1,0:T(1,128)} reshape(f32[1280]{0:T(1024)} %param.8) | data formatting | bytes 10240 | tf_op jit(solution)/shard_map/broadcast_in_dim | solution.py:469
  1.3 1.5 %copy.6.seeds = s32[128,64]{1,0:T(8,128)} copy(s32[128,64]{0,1:T(8,128)} %param.7) | data formatting | bytes 65536 | tf_op args[2]
  2.8 60.5 %shard_map.55 = bf16[128,4096]{1,0:T(8,128)(2,1)} custom-call(s32[128]{0:T(128)} %starts.1, s32[128,64]{1,0:T(8,128)} %copy.6.seeds, f32[1,1280]{1,0:T(1,128)} %broadcast_in_dim.3.gain, bf16[4096,1280]{1,0:T(8,128)(2,1)} %tok_hbm.1, bf16[1280,4096]{1,0:T(8,128)(2,1)} %w_hbm.1), custom_call_target="tpu_custom_call" | custom-call | tf_op jit(solution)/shard_map/pallas_call | solution.py:413
  63.2 2.3 %copy.8 = bf16[128,4096]{1,0:T(8,128)(2,1)} copy(bf16[128,4096]{1,0:T(8,128)(2,1)} %shard_map.55) | data formatting | bytes 2097152

commit v2 on v1

--- a/solution.py
+++ b/solution.py
@@ -15,6 +15,7 @@
 CHUNK = 256
 TILE = 256
 COLS = 512
+LAG = 3
 
 
 def kernel(
@@ -26,21 +27,22 @@
     w_hbm,
     out_hbm,
     x,
+    xt,
     wp,
     outs,
-    s,
+    st,
     wt,
     c,
     po,
     px,
-    pnb,
     si,
     qo,
     tb,
     ub,
     co,
     ci,
-    mn,
+    mf,
+    mx,
     mo,
     mi,
     mq,
@@ -66,8 +68,8 @@
     n_send,
     n_recv,
 ):
-    chunks, rows, _ = x.shape
-    half = rows // 2
+    chunks, _, half, _ = x.shape
+    rows = 2 * half
     tiles = half // TILE
     col_tiles = wp.shape[0]
     width = chunks * CHUNK
@@ -83,9 +85,14 @@
     outer = (outer_seq, 1 - feat)
     h_in, h_out = 1 - feat, feat
 
-    def token_copy(f):
+    def token_copy(f, h):
         return pltpu.make_async_copy(
-            tok_hbm.at[:, pl.ds(pl.multiple_of(f * CHUNK, CHUNK), CHUNK)], x.at[f], x_sem.at[f]
+            tok_hbm.at[
+                pl.ds(pl.multiple_of(h * half, half), half),
+                pl.ds(pl.multiple_of(f * CHUNK, CHUNK), CHUNK),
+            ],
+            x.at[f, h],
+            x_sem.at[f, h],
         )
 
     def weight_copy(n):
@@ -128,7 +135,11 @@
 
     @pl.loop(0, chunks)
     def _(f):
-        token_copy(f).start()
+        token_copy(f, h_in).start()
+
+    @pl.loop(0, chunks)
+    def _(f):
+        token_copy(f, h_out).start()
 
     barrier = pltpu.get_barrier_semaphore()
     pl.semaphore_signal(barrier, inc=1, device_id=inner, device_id_type=MESH)
@@ -139,8 +150,8 @@
 
     base = me * rows
     start = starts[me] - base
-    following = starts[jnp.minimum(me + 1, count - 1)]
-    end = jnp.where(me == count - 1, count * rows, following) - base
+    after = jnp.minimum(me + 1, count - 1)
+    end = jnp.where(me == count - 1, count * rows, starts[after]) - base
 
     def is_mine(shape):
         first = jnp.full(shape, start, jnp.int32) < 0
@@ -155,15 +166,13 @@
         ub[...] = jnp.zeros_like(ub)
         mu[...] = jnp.zeros_like(mu)
 
-    def column(row, offset):
-        spread = jnp.broadcast_to(seeds[pl.ds(row, 1), :].astype(f32), (K, K))
-        return spread.T[:, :1].astype(jnp.int32) + offset
+    def column(shot, offset):
+        shots = lax.broadcasted_iota(jnp.int32, seeds.shape, 1)
+        picked = jnp.where(shots == shot, seeds[...], 0).astype(f32)
+        return jnp.sum(picked, axis=1, keepdims=True).astype(jnp.int32) + offset
 
     own_at = column(me, start)
-    next_at = column(jnp.minimum(me + 1, count - 1), end)
-
-    def lanes(h, t):
-        return lax.broadcasted_iota(jnp.int32, (K, TILE), 1) + (h * half + t * TILE)
+    next_at = column(after, end)
 
     def place(t):
         return pl.ds(pl.multiple_of(t * TILE, TILE), TILE)
@@ -180,51 +189,68 @@
 
     zero = jnp.zeros((K, 128), f32)
 
-    def note_mass(r, nbs, own):
-        def total(m):
-            return jnp.broadcast_to(jnp.sum(m, axis=1, keepdims=True), (K, 128))
-
-        mn[0] = total(nbs[0])
-        mn[1] = total(nbs[1])
-        mo[...] = total(own)
-        mi[r] = mn[h_in]
-        mp_copy(r).start()
-
-    nbs, own_mass = [], zero
-    for h in range(2):
-
-        def seed_tile(t, carry, h=h):
+    def seed_weights(h):
+        def tile(t, carry):
             nb_mass, own_mass = carry
-            at = lanes(h, t)
+            at = lax.broadcasted_iota(jnp.int32, (K, TILE), 1) + (h * half + t * TILE)
             own = (at == own_at).astype(f32)
-            nb = (at == next_at).astype(f32) if h else jnp.zeros((K, TILE), f32)
+            nb = (at == next_at).astype(f32)
             put(h, t, nb, own)
             return nb_mass + fold(nb), own_mass + fold(own)
 
-        nb_mass, own_mass = lax.fori_loop(0, tiles, seed_tile, (zero, own_mass))
-        nbs.append(nb_mass)
+        mf[h, 0], mf[h, 1] = lax.fori_loop(0, tiles, tile, (zero, zero))
+
+    def soften(h):
+        scale = math.log2(math.e) / math.sqrt(width)
+
+        def tile(t, carry):
+            nb_mass, own_mass = carry
+            at = lax.broadcasted_iota(jnp.int32, (1, TILE), 1) + (h * half + t * TILE)
+            is_nb = jnp.logical_or(at < start, at >= end)
+            mixed = jnp.where(is_nb, st[h, :K, place(t)], st[h, K:, place(t)])
+            e = jnp.exp2((mixed - jnp.max(mixed, axis=0, keepdims=True)) * scale)
+            w = e * (1.0 / jnp.sum(e, axis=0, keepdims=True))
+            nb = jnp.where(is_nb, w, 0.0)
+            own = jnp.where(is_nb, 0.0, w)
+            put(h, t, nb, own)
+            return nb_mass + fold(nb), own_mass + fold(own)
+
+        mf[h, 0], mf[h, 1] = lax.fori_loop(0, tiles, tile, (zero, zero), unroll=2)
+
+    seed_weights(h_in)
+    seed_weights(h_out)
 
     pl.semaphore_wait(barrier, 1 + has_outer.astype(jnp.int32))
-
-    note_mass(0, nbs, own_mass)
 
     def wide(m):
         return jnp.concatenate([m] * (CHUNK // 128), axis=1)
 
     def round_body(r, carry):
-        def sums(f):
+        def send_mass():
+            def total(m):
+                return jnp.broadcast_to(jnp.sum(m, axis=1, keepdims=True), (K, 128))
+
+            mi[r] = total(mf[h_in, 0])
+            mp_copy(r).start()
+            mx[...] = total(mf[h_out, 0])
+            mo[...] = total(mf[0, 1] + mf[1, 1])
+
+        def pass_mass_on():
+            mp_copy(r).wait_recv()
+            chip = mo[...] + mq[r]
+            mo[...] = chip
+            mt[r] = jnp.where(is_mine((K, 128)), chip, mx[...])
+
+            @pl.when(has_outer)
+            def _():
+                mt_copy(r).start()
+
+        def partial(f, h):
             @pl.when(r == 0)
             def _():
-                token_copy(f).wait()
-
-            low = jnp.dot(wt[0], x[f, :half], preferred_element_type=f32)
-            high = jnp.dot(wt[1], x[f, half:], preferred_element_type=f32)
-            pnb[0] = low[:K]
-            pnb[1] = high[:K]
-            po[f] = low[K:] + high[K:]
-            px[f] = pnb[h_out]
-            si[r, f] = pnb[h_in]
-            p_copy(r, f).start()
+                token_copy(f, h).wait()
+
+            return jnp.dot(wt[h], x[f, h], preferred_element_type=f32)
 
         def pass_on(f):
             p_copy(r, f).wait_recv()
@@ -236,29 +262,32 @@
             def _():
                 t_copy(r, f).start()
 
-        def pass_mass_on():
-            mp_copy(r).wait_recv()
-            chip = mo[...] + mq[r]
-            mo[...] = chip
-            mt[r] = jnp.where(is_mine((K, 128)), chip, mn[h_out])
-
-            @pl.when(has_outer)
-            def _():
-                mt_copy(r).start()
-
-        @pl.loop(0, chunks + 2)
+        @pl.loop(0, chunks)
+        def _(f):
+            sums = partial(f, h_in)
+            si[r, f] = sums[:K]
+            p_copy(r, f).start()
+            po[f] = sums[K:]
+
+            @pl.when(f == 0)
+            def _():
+                send_mass()
+
+        @pl.loop(0, chunks + 1)
         def _(f):
             @pl.when(f < chunks)
             def _():
-                sums(f)
-
-            @pl.when(f == 2)
+                sums = partial(f, h_out)
+                px[f] = sums[:K]
+                po[f] += sums[K:]
+
+            @pl.when(f == 1)
             def _():
                 pass_mass_on()
 
-            @pl.when(f >= 2)
-            def _():
-                pass_on(f - 2)
+            @pl.when(f >= 1)
+            def _():
+                pass_on(f - 1)
 
         @pl.when(r == 0)
         def _():
@@ -266,7 +295,14 @@
             def _(n):
                 weight_copy(n).start()
 
-        s[...] = jnp.zeros_like(s)
+            @pl.loop(0, chunks)
+            def _(f):
+                for h in range(2):
+                    for t in range(tiles):
+                        at = slice(t * TILE, (t + 1) * TILE)
+                        xt[f, h, :, at] = x[f, h, at].T
+
+        st[...] = jnp.zeros_like(st)
 
         @pl.when(has_outer)
         def _():
@@ -274,7 +310,7 @@
 
         mine = is_mine((K, 128))
         m_own = mo[...] + jnp.where(mine, mu[r], 0.0)
-        m_nb = mn[h_out] + jnp.where(mine, 0.0, mu[r])
+        m_nb = mx[...] + jnp.where(mine, 0.0, mu[r])
         rec[0] = 1.0 / m_own
         rec[1] = 1.0 / jnp.where(m_nb > 0.0, m_nb, 1.0)
 
@@ -287,64 +323,45 @@
             u = ub[r, f].astype(f32)
             own = (po[f] + jnp.where(mine, u, 0.0)) * wide(rec[0])
             cent[f] = own
-            return (px[f] + jnp.where(mine, 0.0, u)) * wide(rec[1])
+            return own, (px[f] + jnp.where(mine, 0.0, u)) * wide(rec[1])
 
         def spread(f):
-            nb = arrive(f)
-            own = cent[f].astype(bf16)
+            own, nb = arrive(f)
+            own = own.astype(bf16)
             co[r, f] = own
             c_copy(r, f).start()
             c[0, f, K:] = own
             c[1, f, K:] = own
             c[h_out, f, :K] = nb.astype(bf16)
 
-        def score(f):
+        def score(f, h):
+            for t in range(half // COLS):
+                at = slice(t * COLS, (t + 1) * COLS)
+                st[h, :, at] += jnp.dot(c[h, f], xt[f, h, :, at], preferred_element_type=f32)
+
+        def score_inner(f):
             c_copy(r, f).wait_recv()
             c[h_in, f, :K] = ci[r, f]
-            for h in range(2):
-                s[h * half : (h + 1) * half] += lax.dot_general(
-                    x[f, h * half : (h + 1) * half],
-                    c[h, f],
-                    (((1,), (1,)), ((), ())),
-                    preferred_element_type=f32,
-                )
-
-        def soften():
-            scale = math.log2(math.e) / math.sqrt(width)
-            nbs, own_mass = [], zero
-            for h in range(2):
-
-                def tile(t, carry, h=h):
-                    nb_mass, own_mass = carry
-                    at = pl.ds(pl.multiple_of(h * half + t * TILE, TILE), TILE)
-                    flat = s[at].T
-                    where = lanes(h, t)
-                    is_nb = (where >= end) if h else (where < start)
-                    mixed = jnp.where(is_nb, flat[:K], flat[K:])
-                    e = jnp.exp2((mixed - jnp.max(mixed, axis=0, keepdims=True)) * scale)
-                    w = e * (1.0 / jnp.sum(e, axis=0, keepdims=True))
-                    nb = jnp.where(is_nb, w, 0.0)
-                    own = jnp.where(is_nb, 0.0, w)
-                    put(h, t, nb, own)
-                    return nb_mass + fold(nb), own_mass + fold(own)
-
-                nb_mass, own_mass = lax.fori_loop(0, tiles, tile, (zero, own_mass))
-                nbs.append(nb_mass)
-            note_mass(r + 1, nbs, own_mass)
+            score(f, h_in)
 
         @pl.when(r < ITERS)
         def _():
-            @pl.loop(0, chunks + 2)
+            @pl.loop(0, chunks)
             def _(f):
-                @pl.when(f < chunks)
+                spread(f)
+                score(f, h_out)
+
+                @pl.when(f >= LAG)
                 def _():
-                    spread(f)
-
-                @pl.when(f >= 2)
-                def _():
-                    score(f - 2)
-
-            soften()
+                    score_inner(f - LAG)
+
+            soften(h_out)
+
+            @pl.loop(chunks - LAG, chunks)
+            def _(f):
+                score_inner(f)
+
+            soften(h_in)
 
         @pl.when(r == ITERS)
         def _():
@@ -362,7 +379,7 @@
     inverse = 1.0 / jnp.sqrt(square / width + 1e-06)
     for f in range(chunks):
         at = slice(f * CHUNK, (f + 1) * CHUNK)
-        normed = (cent[f] * inverse * gain[:, at]).astype(bf16)
+        normed = (cent[f] * inverse * gain[at][None, :]).astype(bf16)
         ns[:, at] = normed
         nm[pl.ds(pl.multiple_of(feat * K, K), K), at] = normed
     n_copy().start()
@@ -422,22 +439,23 @@
         ],
         out_specs=pl.BlockSpec(memory_space=pl.ANY),
         scratch_shapes=[
-            vmem((chunks, rows, CHUNK), bf16),
+            vmem((chunks, 2, half, CHUNK), bf16),
+            vmem((chunks, 2, CHUNK, half), bf16),
             vmem((col_tiles, width, COLS), bf16),
             vmem((col_tiles, 2 * K, COLS), bf16),
-            vmem((rows, 2 * K), f32),
+            vmem((2, 2 * K, half), f32),
             vmem((2, 2 * K, half), bf16),
             vmem((2, chunks, 2 * K, CHUNK), bf16),
             vmem((chunks, *piece), f32),
             vmem((chunks, *piece), f32),
-            vmem((2, *piece), f32),
             vmem((ROUNDS, chunks, *piece), f32),
             vmem((ROUNDS, chunks, *piece), f32),
             vmem((ROUNDS, chunks, *piece), bf16),
             vmem((ROUNDS, chunks, *piece), bf16),
             vmem((ITERS, chunks, *piece), bf16),
             vmem((ITERS, chunks, *piece), bf16),
-            vmem((2, K, 128), f32),
+            vmem((2, 2, K, 128), f32),
+            vmem((K, 128), f32),
             vmem((K, 128), f32),
             vmem((ROUNDS, K, 128), f32),
             vmem((ROUNDS, K, 128), f32),
@@ -447,7 +465,7 @@
             vmem((chunks, *piece), f32),
             vmem((K, width), bf16),
             vmem((2 * K, width), bf16),
-            dma((chunks,)),
+            dma((chunks, 2)),
             dma((col_tiles,)),
             dma((col_tiles,)),
             dma((ROUNDS, chunks)),
@@ -466,7 +484,7 @@
         compiler_params=pltpu.CompilerParams(
             collective_id=0, has_side_effects=True, vmem_limit_bytes=60 * 2**20
         ),
-    )(shot_starts, seed_offsets, norm_gain[None, :], tokens, proj_weight)
+    )(shot_starts, seed_offsets.T, norm_gain, tokens, proj_weight)
 
 
 def solution(mesh):

time: 65.8 us -> 57.1 us (0.87)
  Pallas kernels: 60.5 us -> 54.6 us
  local copies, waits for them, and re-layouts: 5.06 us -> 2.29 us
    pallas_call x1, Pallas kernels: 60.5 us -> 54.6 us  [on_device(): pl.pallas_call(functools.partial(kernel, seq_size), out_shape=jax.ShapeDt...]
    unnamed x2 -> x1, local copies, waits for them, and re-layouts: 3.77 us -> 2.29 us
    broadcast_in_dim x1 -> x0, local copies, waits for them, and re-layouts: 1.29 us -> none  [on_device(): norm_gain[None, :]]
where the time goes in v2:
time: 57.1 us; the launch traced here: 56.9 us
  Pallas kernels  54.6 us (96%)
  local copies, waits for them, and re-layouts  2.29 us (4%)
    pallas_call x1, Pallas kernels, on_device(): pl.pallas_call(functools.partial(kernel, seq_size), out_shape=jax.ShapeDt...  54.6 us
    unnamed x1, local copies, waits for them, and re-layouts  2.29 us

profile of v2, /device:TPU:97, one launch (start us, length us, event | category | flops | bytes accessed | tf_op | source)
XLA Modules:
  0.0 56.9 jit_solution(7073237327858273702)
XLA Ops:
  0.0 54.6 %shard_map.55 = bf16[128,4096]{1,0:T(8,128)(2,1)} custom-call(s32[128]{0:T(128)} %starts.1, s32[64,128]{1,0:T(8,128)} %bitcast.1, f32[1280]{0:T(1024)} %gain.1, bf16[4096,1280]{1,0:T(8,128)(2,1)} %tok_hbm.1, bf16[1280,4096]{1,0:T(8,128)(2,1)} %w_hbm.1), custom_call_target="tpu_custom_call" | custom-call | tf_op jit(solution)/shard_map/pallas_call | solution.py:430
  54.6 2.3 %copy.7 = bf16[128,4096]{1,0:T(8,128)(2,1)} copy(bf16[128,4096]{1,0:T(8,128)(2,1)} %shard_map.55) | data formatting | bytes 2097152

commit v3 on v2

v3 whole, which is shorter than its diff:
```python
import functools
import math

import jax
import jax.numpy as jnp
from jax import lax
from jax.experimental import pallas as pl
from jax.experimental.pallas import tpu as pltpu
from jax.sharding import PartitionSpec as P

MESH = pl.DeviceIdType.MESH
ITERS = 3
ROUNDS = ITERS + 1
K = 64
CHUNK = 256
TILE = 256
COLS = 512
GROUPS = ((0, 1), (2, 3), (4,))


def kernel(
    seq_size,
    starts,
    seeds,
    gain,
    tok_hbm,
    w_hbm,
    out_hbm,
    x,
    xt,
    wp,
    outs,
    st,
    wt,
    c,
    po,
    px,
    si,
    qo,
    tb,
    ub,
    co,
    ci,
    mf,
    mx,
    mo,
    mi,
    mq,
    mt,
    mu,
    rec,
    cent,
    ns,
    nm,
    x_sem,
    w_sem,
    o_sem,
    p_send,
    p_recv,
    t_send,
    t_recv,
    c_send,
    c_recv,
    mp_send,
    mp_recv,
    mt_send,
    mt_recv,
    n_send,
    n_recv,
):
    chunks, _, half, _ = x.shape
    rows = 2 * half
    tiles = half // TILE
    col_tiles = wp.shape[0]
    width = chunks * CHUNK
    f32, bf16 = jnp.float32, jnp.bfloat16

    seq = lax.axis_index("seq")
    feat = lax.axis_index("feat")
    me = seq * 2 + feat
    count = seq_size * 2
    inner = (seq, 1 - feat)
    outer_seq = seq + 2 * feat - 1
    has_outer = jnp.logical_and(outer_seq >= 0, outer_seq < seq_size)
    outer = (outer_seq, 1 - feat)
    h_in, h_out = 1 - feat, feat

    def token_copy(f, h):
        return pltpu.make_async_copy(
            tok_hbm.at[
                pl.ds(pl.multiple_of(h * half, half), half),
                pl.ds(pl.multiple_of(f * CHUNK, CHUNK), CHUNK),
            ],
            x.at[f, h],
            x_sem.at[f, h],
        )

    def weight_copy(n):
        return pltpu.make_async_copy(
            w_hbm.at[:, pl.ds(pl.multiple_of(n * COLS, COLS), COLS)], wp.at[n], w_sem.at[n]
        )

    def out_copy(n):
        return pltpu.make_async_copy(
            outs.at[n], out_hbm.at[:, pl.ds(pl.multiple_of(n * COLS, COLS), COLS)], o_sem.at[n]
        )

    def remote(src, dst, send, recv, device):
        return pltpu.make_async_remote_copy(
            src_ref=src,
            dst_ref=dst,
            send_sem=send,
            recv_sem=recv,
            device_id=device,
            device_id_type=MESH,
        )

    def p_copy(r, g):
        at = pl.ds(GROUPS[g][0], len(GROUPS[g]))
        return remote(si.at[r, at], qo.at[r, at], p_send.at[r, g], p_recv.at[r, g], inner)

    def t_copy(r, g):
        at = pl.ds(GROUPS[g][0], len(GROUPS[g]))
        return remote(tb.at[r, at], ub.at[r, at], t_send.at[r, g], t_recv.at[r, g], outer)

    def c_copy(r, g):
        at = pl.ds(GROUPS[g][0], len(GROUPS[g]))
        return remote(co.at[r, at], ci.at[r, at], c_send.at[r, g], c_recv.at[r, g], inner)

    def mp_copy(r):
        return remote(mi.at[r], mq.at[r], mp_send.at[r], mp_recv.at[r], inner)

    def mt_copy(r):
        return remote(mt.at[r], mu.at[r], mt_send.at[r], mt_recv.at[r], outer)

    def n_copy():
        return remote(ns, nm.at[pl.ds(feat * K, K)], n_send, n_recv, inner)

    for f in range(chunks):
        token_copy(f, h_in).start()
    for f in range(chunks):
        token_copy(f, h_out).start()

    barrier = pltpu.get_barrier_semaphore()
    pl.semaphore_signal(barrier, inc=1, device_id=inner, device_id_type=MESH)

    @pl.when(has_outer)
    def _():
        pl.semaphore_signal(barrier, inc=1, device_id=outer, device_id_type=MESH)

    base = me * rows
    start = starts[me] - base
    after = jnp.minimum(me + 1, count - 1)
    end = jnp.where(me == count - 1, count * rows, starts[after]) - base

    def is_mine(shape):
        first = jnp.full(shape, start, jnp.int32) < 0
        last = jnp.full(shape, end, jnp.int32) >= rows
        left = jnp.full(shape, feat, jnp.int32) == 0
        return jnp.logical_or(
            jnp.logical_and(left, first), jnp.logical_and(jnp.logical_not(left), last)
        )

    @pl.when(jnp.logical_not(has_outer))
    def _():
        ub[...] = jnp.zeros_like(ub)
        mu[...] = jnp.zeros_like(mu)

    def column(shot, offset):
        shots = lax.broadcasted_iota(jnp.int32, seeds.shape, 1)
        picked = jnp.where(shots == shot, seeds[...], 0).astype(f32)
        return jnp.sum(picked, axis=1, keepdims=True).astype(jnp.int32) + offset

    own_at = column(me, start)
    next_at = column(after, end)

    def place(t):
        return slice(t * TILE, (t + 1) * TILE)

    def fold(w):
        total = w[:, :128]
        for i in range(1, TILE // 128):
            total = total + w[:, i * 128 : (i + 1) * 128]
        return total

    def put(h, t, nb, own):
        wt[h, :K, place(t)] = nb.astype(bf16)
        wt[h, K:, place(t)] = own.astype(bf16)

    def seed_weights(h):
        nb_mass, own_mass = 0.0, 0.0
        for t in range(tiles):
            at = lax.broadcasted_iota(jnp.int32, (K, TILE), 1) + (h * half + t * TILE)
            own = (at == own_at).astype(f32)
            nb = (at == next_at).astype(f32)
            put(h, t, nb, own)
            nb_mass, own_mass = nb_mass + fold(nb), own_mass + fold(own)
        mf[h, 0], mf[h, 1] = nb_mass, own_mass

    def group_score(group, h, at):
        total = 0.0
        for f in group:
            total = total + jnp.dot(c[h, f], xt[f, h, :, at], preferred_element_type=f32)
        return total

    def soften(h):
        scale = math.log2(math.e) / math.sqrt(width)
        nb_mass, own_mass = 0.0, 0.0
        for t in range(tiles):
            scores = st[h, :, place(t)] + group_score(GROUPS[-1], h, place(t))
            at = lax.broadcasted_iota(jnp.int32, (1, TILE), 1) + (h * half + t * TILE)
            is_nb = jnp.logical_or(at < start, at >= end)
            mixed = jnp.where(is_nb, scores[:K], scores[K:])
            e = jnp.exp2((mixed - jnp.max(mixed, axis=0, keepdims=True)) * scale)
            w = e * (1.0 / jnp.sum(e, axis=0, keepdims=True))
            nb = jnp.where(is_nb, w, 0.0)
            own = jnp.where(is_nb, 0.0, w)
            put(h, t, nb, own)
            nb_mass, own_mass = nb_mass + fold(nb), own_mass + fold(own)
        mf[h, 0], mf[h, 1] = nb_mass, own_mass

    def wide(m):
        return jnp.concatenate([m] * (CHUNK // 128), axis=1)

    def total_mass(m):
        return jnp.broadcast_to(jnp.sum(m, axis=1, keepdims=True), (K, 128))

    def sum_and_send(r, first):
        def partial(f, h):
            if first:
                token_copy(f, h).wait()
            return jnp.dot(wt[h], x[f, h], preferred_element_type=f32)

        for g, group in enumerate(GROUPS):
            for f in group:
                sums = partial(f, h_in)
                si[r, f] = sums[:K].astype(bf16)
                po[f] = sums[K:]
            if g == 0:
                mi[r] = total_mass(mf[h_in, 0])
                mp_copy(r).start()
            p_copy(r, g).start()
            if g == 0:
                mx[...] = total_mass(mf[h_out, 0])
                mo[...] = total_mass(mf[0, 1] + mf[1, 1])

        for g, group in enumerate(GROUPS):
            for f in group:
                sums = partial(f, h_out)
                px[f] = sums[:K]
                po[f] += sums[K:]
            if g == 0:
                mp_copy(r).wait_recv()
                chip = mo[...] + mq[r]
                mo[...] = chip
                mt[r] = jnp.where(is_mine((K, 128)), chip, mx[...])
            p_copy(r, g).wait_recv()
            for f in group:
                chip = po[f] + qo[r, f].astype(f32)
                po[f] = chip
                tb[r, f] = jnp.where(is_mine((K, CHUNK)), chip, px[f]).astype(bf16)

            @pl.when(has_outer)
            def _():
                if g == 0:
                    mt_copy(r).start()
                t_copy(r, g).start()

    def take_mass(r):
        @pl.when(has_outer)
        def _():
            mt_copy(r).wait_recv()

        mine = is_mine((K, 128))
        m_nb = mx[...] + jnp.where(mine, 0.0, mu[r])
        rec[0] = 1.0 / (mo[...] + jnp.where(mine, mu[r], 0.0))
        rec[1] = 1.0 / jnp.where(m_nb > 0.0, m_nb, 1.0)

    def arrive(r, g):
        @pl.when(has_outer)
        def _():
            t_copy(r, g).wait_recv()

    def own_total(r, f):
        return (
            po[f] + jnp.where(is_mine((K, CHUNK)), ub[r, f].astype(f32), 0.0)
        ) * wide(rec[0])

    def outer_total(r, f):
        return (
            px[f] + jnp.where(is_mine((K, CHUNK)), 0.0, ub[r, f].astype(f32))
        ) * wide(rec[1])

    def spread(r, g):
        arrive(r, g)
        for f in GROUPS[g]:
            own = own_total(r, f).astype(bf16)
            co[r, f] = own
            c[0, f, K:] = own
            c[1, f, K:] = own
        c_copy(r, g).start()
        for f in GROUPS[g]:
            c[h_out, f, :K] = outer_total(r, f).astype(bf16)

    def score(g, h):
        if g == len(GROUPS) - 1:
            soften(h)
            return
        for t in range(half // COLS):
            at = slice(t * COLS, (t + 1) * COLS)
            scores = group_score(GROUPS[g], h, at)
            if g:
                scores = scores + st[h, :, at]
            st[h, :, at] = scores

    def score_inner(r, g):
        c_copy(r, g).wait_recv()
        for f in GROUPS[g]:
            c[h_in, f, :K] = ci[r, f]
        score(g, h_in)

    seed_weights(h_in)
    seed_weights(h_out)
    pl.semaphore_wait(barrier, 1 + has_outer.astype(jnp.int32))
    sum_and_send(0, True)

    for n in range(col_tiles):
        weight_copy(n).start()

    @pl.loop(0, chunks)
    def _(f):
        for h in range(2):
            for t in range(tiles):
                xt[f, h, :, place(t)] = x[f, h, place(t)].T

    @pl.loop(0, ITERS)
    def _(r):
        take_mass(r)
        for g in range(len(GROUPS)):
            spread(r, g)
            score(g, h_out)
            if g:
                score_inner(r, g - 1)
        score_inner(r, len(GROUPS) - 1)
        sum_and_send(r + 1, False)

    take_mass(ITERS)
    square = jnp.zeros((K, 1), f32)
    for g, group in enumerate(GROUPS):
        arrive(ITERS, g)
        for f in group:
            own = own_total(ITERS, f)
            cent[f] = own
            square = square + jnp.sum(own * own, axis=1, keepdims=True)
    inverse = 1.0 / jnp.sqrt(square / width + 1e-06)
    for f in range(chunks):
        at = slice(f * CHUNK, (f + 1) * CHUNK)
        normed = (cent[f] * inverse * gain[at][None, :]).astype(bf16)
        ns[:, at] = normed
        nm[pl.ds(pl.multiple_of(feat * K, K), K), at] = normed
    n_copy().start()
    for n in range(col_tiles):
        weight_copy(n).wait()
    n_copy().wait_recv()

    for n in range(col_tiles):
        outs[n] = jnp.dot(nm[...], wp[n], preferred_element_type=f32).astype(bf16)
        if n % 2:
            out_copy(n - 1).start()
            out_copy(n).start()

    n_copy().wait_send()

    @pl.loop(0, ROUNDS)
    def _(r):
        mp_copy(r).wait_send()
        for g in range(len(GROUPS)):
            p_copy(r, g).wait_send()

        @pl.when(r < ITERS)
        def _():
            for g in range(len(GROUPS)):
                c_copy(r, g).wait_send()

        @pl.when(has_outer)
        def _():
            mt_copy(r).wait_send()
            for g in range(len(GROUPS)):
                t_copy(r, g).wait_send()

    for n in range(col_tiles):
        out_copy(n).wait()


def on_device(seq_size, tokens, shot_starts, seed_offsets, norm_gain, proj_weight):
    rows, width = tokens.shape
    columns = proj_weight.shape[1]
    chunks = width // CHUNK
    col_tiles = columns // COLS
    half = rows // 2
    f32, bf16 = jnp.float32, jnp.bfloat16
    vmem, dma = pltpu.VMEM, pltpu.SemaphoreType.DMA
    piece = (K, CHUNK)
    return pl.pallas_call(
        functools.partial(kernel, seq_size),
        out_shape=jax.ShapeDtypeStruct((2 * K, columns), bf16),
        in_specs=[
            pl.BlockSpec(memory_space=pltpu.SMEM),
            pl.BlockSpec(memory_space=pltpu.VMEM),
            pl.BlockSpec(memory_space=pltpu.VMEM),
            pl.BlockSpec(memory_space=pl.ANY),
            pl.BlockSpec(memory_space=pl.ANY),
        ],
        out_specs=pl.BlockSpec(memory_space=pl.ANY),
        scratch_shapes=[
            vmem((chunks, 2, half, CHUNK), bf16),
            vmem((chunks, 2, CHUNK, half), bf16),
            vmem((col_tiles, width, COLS), bf16),
            vmem((col_tiles, 2 * K, COLS), bf16),
            vmem((2, 2 * K, half), f32),
            vmem((2, 2 * K, half), bf16),
            vmem((2, chunks, 2 * K, CHUNK), bf16),
            vmem((chunks, *piece), f32),
            vmem((chunks, *piece), f32),
            vmem((ROUNDS, chunks, *piece), bf16),
            vmem((ROUNDS, chunks, *piece), bf16),
            vmem((ROUNDS, chunks, *piece), bf16),
            vmem((ROUNDS, chunks, *piece), bf16),
            vmem((ITERS, chunks, *piece), bf16),
            vmem((ITERS, chunks, *piece), bf16),
            vmem((2, 2, K, 128), f32),
            vmem((K, 128), f32),
            vmem((K, 128), f32),
            vmem((ROUNDS, K, 128), f32),
            vmem((ROUNDS, K, 128), f32),
            vmem((ROUNDS, K, 128), f32),
            vmem((ROUNDS, K, 128), f32),
            vmem((2, K, 128), f32),
            vmem((chunks, *piece), f32),
            vmem((K, width), bf16),
            vmem((2 * K, width), bf16),
            dma((chunks, 2)),
            dma((col_tiles,)),
            dma((col_tiles,)),
            dma((ROUNDS, len(GROUPS))),
            dma((ROUNDS, len(GROUPS))),
            dma((ROUNDS, len(GROUPS))),
            dma((ROUNDS, len(GROUPS))),
            dma((ITERS, len(GROUPS))),
            dma((ITERS, len(GROUPS))),
            dma((ROUNDS,)),
            dma((ROUNDS,)),
            dma((ROUNDS,)),
            dma((ROUNDS,)),
            dma,
            dma,
        ],
        compiler_params=pltpu.CompilerParams(
            collective_id=0, has_side_effects=True, vmem_limit_bytes=60 * 2**20
        ),
    )(shot_starts, seed_offsets.T, norm_gain, tokens, proj_weight)


def solution(mesh):
    in_specs = (P(("seq", "feat"), None), P(), P(), P(), P(None, "feat"))
    out_specs = P("seq", "feat")
    return jax.shard_map(
        functools.partial(on_device, mesh.shape["seq"]),
        mesh=mesh,
        in_specs=in_specs,
        out_specs=out_specs,
        check_vma=False,
    )
```

time: 57.1 us -> 52.1 us (0.912)
  Pallas kernels: 54.6 us -> 49.6 us
    pallas_call x1, Pallas kernels: 54.6 us -> 49.6 us  [on_device(): pl.pallas_call(functools.partial(kernel, seq_size), out_shape=jax.ShapeDt...]
where the time goes in v3:
time: 52.1 us; the launch traced here: 51.9 us
  Pallas kernels  49.6 us (95%)
  local copies, waits for them, and re-layouts  2.29 us (4%)
    pallas_call x1, Pallas kernels, on_device(): pl.pallas_call(functools.partial(kernel, seq_size), out_shape=jax.ShapeDt...  49.6 us
    unnamed x1, local copies, waits for them, and re-layouts  2.29 us

profile of v3, /device:TPU:97, one launch (start us, length us, event | category | flops | bytes accessed | tf_op | source)
XLA Modules:
  0.0 51.9 jit_solution(6080319184402157021)
XLA Ops:
  0.0 49.6 %shard_map.55 = bf16[128,4096]{1,0:T(8,128)(2,1)} custom-call(s32[128]{0:T(128)} %starts.1, s32[64,128]{1,0:T(8,128)} %bitcast.1, f32[1280]{0:T(1024)} %gain.1, bf16[4096,1280]{1,0:T(8,128)(2,1)} %tok_hbm.1, bf16[1280,4096]{1,0:T(8,128)(2,1)} %w_hbm.1), custom_call_target="tpu_custom_call" | custom-call | tf_op jit(solution)/shard_map/pallas_call | solution.py:404
  49.6 2.3 %copy.7 = bf16[128,4096]{1,0:T(8,128)(2,1)} copy(bf16[128,4096]{1,0:T(8,128)(2,1)} %shard_map.55) | data formatting | bytes 2097152

commit v4 on v3

--- a/solution.py
+++ b/solution.py
@@ -15,7 +15,7 @@
 CHUNK = 256
 TILE = 256
 COLS = 512
-GROUPS = ((0, 1), (2, 3), (4,))
+GROUPS = ((0, 1), (2, 3, 4))
 
 
 def kernel(
@@ -25,11 +25,10 @@
     gain,
     tok_hbm,
     w_hbm,
-    out_hbm,
+    nm,
+    wp,
     x,
     xt,
-    wp,
-    outs,
     st,
     wt,
     c,
@@ -51,10 +50,9 @@
     rec,
     cent,
     ns,
-    nm,
+    nr,
     x_sem,
     w_sem,
-    o_sem,
     p_send,
     p_recv,
     t_send,
@@ -100,11 +98,6 @@
             w_hbm.at[:, pl.ds(pl.multiple_of(n * COLS, COLS), COLS)], wp.at[n], w_sem.at[n]
         )
 
-    def out_copy(n):
-        return pltpu.make_async_copy(
-            outs.at[n], out_hbm.at[:, pl.ds(pl.multiple_of(n * COLS, COLS), COLS)], o_sem.at[n]
-        )
-
     def remote(src, dst, send, recv, device):
         return pltpu.make_async_remote_copy(
             src_ref=src,
@@ -134,7 +127,7 @@
         return remote(mt.at[r], mu.at[r], mt_send.at[r], mt_recv.at[r], outer)
 
     def n_copy():
-        return remote(ns, nm.at[pl.ds(feat * K, K)], n_send, n_recv, inner)
+        return remote(ns, nr, n_send, n_recv, inner)
 
     for f in range(chunks):
         token_copy(f, h_in).start()
@@ -362,12 +355,7 @@
     for n in range(col_tiles):
         weight_copy(n).wait()
     n_copy().wait_recv()
-
-    for n in range(col_tiles):
-        outs[n] = jnp.dot(nm[...], wp[n], preferred_element_type=f32).astype(bf16)
-        if n % 2:
-            out_copy(n - 1).start()
-            out_copy(n).start()
+    nm[pl.ds(pl.multiple_of((1 - feat) * K, K), K)] = nr[...]
 
     n_copy().wait_send()
 
@@ -388,6 +376,19 @@
             for g in range(len(GROUPS)):
                 t_copy(r, g).wait_send()
 
+
+def project(nm, wp, out_hbm, outs, o_sem):
+    def out_copy(n):
+        return pltpu.make_async_copy(
+            outs.at[n], out_hbm.at[:, pl.ds(n * COLS, COLS)], o_sem.at[n]
+        )
+
+    col_tiles = wp.shape[0]
+    for n in range(col_tiles):
+        outs[n] = jnp.dot(nm[...], wp[n], preferred_element_type=jnp.float32).astype(jnp.bfloat16)
+        if n % 2:
+            out_copy(n - 1).start()
+            out_copy(n).start()
     for n in range(col_tiles):
         out_copy(n).wait()
 
@@ -401,9 +402,9 @@
     f32, bf16 = jnp.float32, jnp.bfloat16
     vmem, dma = pltpu.VMEM, pltpu.SemaphoreType.DMA
     piece = (K, CHUNK)
-    return pl.pallas_call(
+    normed, weights = pl.pallas_call(
         functools.partial(kernel, seq_size),
-        out_shape=jax.ShapeDtypeStruct((2 * K, columns), bf16),
+        out_shape=(vmem((2 * K, width), bf16), vmem((col_tiles, width, COLS), bf16)),
         in_specs=[
             pl.BlockSpec(memory_space=pltpu.SMEM),
             pl.BlockSpec(memory_space=pltpu.VMEM),
@@ -411,12 +412,10 @@
             pl.BlockSpec(memory_space=pl.ANY),
             pl.BlockSpec(memory_space=pl.ANY),
         ],
-        out_specs=pl.BlockSpec(memory_space=pl.ANY),
+        out_specs=(pl.BlockSpec(memory_space=pltpu.VMEM),) * 2,
         scratch_shapes=[
             vmem((chunks, 2, half, CHUNK), bf16),
             vmem((chunks, 2, CHUNK, half), bf16),
-            vmem((col_tiles, width, COLS), bf16),
-            vmem((col_tiles, 2 * K, COLS), bf16),
             vmem((2, 2 * K, half), f32),
             vmem((2, 2 * K, half), bf16),
             vmem((2, chunks, 2 * K, CHUNK), bf16),
@@ -438,9 +437,8 @@
             vmem((2, K, 128), f32),
             vmem((chunks, *piece), f32),
             vmem((K, width), bf16),
-            vmem((2 * K, width), bf16),
+            vmem((K, width), bf16),
             dma((chunks, 2)),
-            dma((col_tiles,)),
             dma((col_tiles,)),
             dma((ROUNDS, len(GROUPS))),
             dma((ROUNDS, len(GROUPS))),
@@ -456,9 +454,17 @@
             dma,
         ],
         compiler_params=pltpu.CompilerParams(
-            collective_id=0, has_side_effects=True, vmem_limit_bytes=60 * 2**20
+            collective_id=0, has_side_effects=True, vmem_limit_bytes=46 * 2**20
         ),
     )(shot_starts, seed_offsets.T, norm_gain, tokens, proj_weight)
+    return pl.pallas_call(
+        project,
+        out_shape=jax.ShapeDtypeStruct((2 * K, columns), bf16),
+        in_specs=[pl.BlockSpec(memory_space=pltpu.VMEM)] * 2,
+        out_specs=pl.BlockSpec(memory_space=pl.ANY),
+        scratch_shapes=[vmem((col_tiles, 2 * K, COLS), bf16), dma((col_tiles,))],
+        compiler_params=pltpu.CompilerParams(vmem_limit_bytes=20 * 2**20),
+    )(normed, weights)
 
 
 def solution(mesh):

time: 52.1 us -> 48.2 us (0.925)
  local copies, waits for them, and re-layouts: 2.29 us -> 0 us
  Pallas kernels: 49.6 us -> 48 us
    unnamed x1 -> x0, local copies, waits for them, and re-layouts: 2.29 us -> none
    pallas_call x1 -> x2, Pallas kernels: 49.6 us -> 48 us  [the longest x1 45.7 us: on_device(): pl.pallas_call(functools.partial(kernel, seq_size), out_shape=(vmem((2 *...]
where the time goes in v4:
time: 48.2 us; the launch traced here: 48 us
  Pallas kernels  48 us (100%)
    pallas_call x1, Pallas kernels, on_device(): pl.pallas_call(functools.partial(kernel, seq_size), out_shape=(vmem((2 *...  45.7 us
    pallas_call x1, Pallas kernels, on_device(): pl.pallas_call(project, out_shape=jax.ShapeDtypeStruct((2 * K, columns),...  2.31 us

profile of v4, /device:TPU:97, one launch (start us, length us, event | category | flops | bytes accessed | tf_op | source)
XLA Modules:
  0.0 48.0 jit_solution(13663533718620920723)
XLA Ops:
  0.0 45.7 %shard_map.55 = (bf16[128,1280]{1,0:T(8,128)(2,1)S(1)}, bf16[8,1280,512]{2,1,0:T(8,128)(2,1)S(1)}) custom-call(s32[128]{0:T(128)} %starts.1, s32[64,128]{1,0:T(8,128)} %bitcast.1, f32[1280]{0:T(1024)} %gain.1, bf16[4096,1280]{1,0:T(8,128)(2,1)} %tok_hbm.1, bf16[1280,4096]{1,0:T(8,128)(2,1)} %w_hbm.1), custom_call_target="tpu_custom_call" | custom-call | tf_op jit(solution)/shard_map/pallas_call | solution.py:405
  45.7 2.3 %shard_map.56 = bf16[128,4096]{1,0:T(8,128)(2,1)} custom-call(bf16[128,1280]{1,0:T(8,128)(2,1)S(1)} %get-tuple-element.7.nm, bf16[8,1280,512]{2,1,0:T(8,128)(2,1)S(1)} %get-tuple-element.8.wp), custom_call_target="tpu_custom_call" | custom-call | tf_op jit(solution)/shard_map/pallas_call | solution.py:460

commit v5 on v4

--- a/solution.py
+++ b/solution.py
@@ -15,7 +15,7 @@
 CHUNK = 256
 TILE = 256
 COLS = 512
-GROUPS = ((0, 1), (2, 3, 4))
+GROUPS = ((0,), (1, 2), (3, 4))
 
 
 def kernel(
@@ -205,9 +205,9 @@
             is_nb = jnp.logical_or(at < start, at >= end)
             mixed = jnp.where(is_nb, scores[:K], scores[K:])
             e = jnp.exp2((mixed - jnp.max(mixed, axis=0, keepdims=True)) * scale)
-            w = e * (1.0 / jnp.sum(e, axis=0, keepdims=True))
-            nb = jnp.where(is_nb, w, 0.0)
-            own = jnp.where(is_nb, 0.0, w)
+            share = 1.0 / jnp.sum(e, axis=0, keepdims=True)
+            nb = e * jnp.where(is_nb, share, 0.0)
+            own = e * jnp.where(is_nb, 0.0, share)
             put(h, t, nb, own)
             nb_mass, own_mass = nb_mass + fold(nb), own_mass + fold(own)
         mf[h, 0], mf[h, 1] = nb_mass, own_mass
@@ -218,17 +218,25 @@
     def total_mass(m):
         return jnp.broadcast_to(jnp.sum(m, axis=1, keepdims=True), (K, 128))
 
+    def partial(f, h, first=False):
+        if first:
+            token_copy(f, h).wait()
+        return jnp.dot(wt[h], x[f, h], preferred_element_type=f32)
+
+    def sum_early():
+        for f in GROUPS[0]:
+            sums = partial(f, h_out)
+            px[f] = sums[:K]
+            po[f] = sums[K:]
+
     def sum_and_send(r, first):
-        def partial(f, h):
-            if first:
-                token_copy(f, h).wait()
-            return jnp.dot(wt[h], x[f, h], preferred_element_type=f32)
-
         for g, group in enumerate(GROUPS):
             for f in group:
-                sums = partial(f, h_in)
+                sums = partial(f, h_in, first)
                 si[r, f] = sums[:K].astype(bf16)
-                po[f] = sums[K:]
+                po[f] = sums[K:] if g or first else po[f] + sums[K:]
+            if first and g == 0:
+                pl.semaphore_wait(barrier, 1 + has_outer.astype(jnp.int32))
             if g == 0:
                 mi[r] = total_mass(mf[h_in, 0])
                 mp_copy(r).start()
@@ -238,8 +246,8 @@
                 mo[...] = total_mass(mf[0, 1] + mf[1, 1])
 
         for g, group in enumerate(GROUPS):
-            for f in group:
-                sums = partial(f, h_out)
+            for f in group if g or first else ():
+                sums = partial(f, h_out, first)
                 px[f] = sums[:K]
                 po[f] += sums[K:]
             if g == 0:
@@ -314,7 +322,6 @@
 
     seed_weights(h_in)
     seed_weights(h_out)
-    pl.semaphore_wait(barrier, 1 + has_outer.astype(jnp.int32))
     sum_and_send(0, True)
 
     for n in range(col_tiles):
@@ -334,6 +341,7 @@
             score(g, h_out)
             if g:
                 score_inner(r, g - 1)
+        sum_early()
         score_inner(r, len(GROUPS) - 1)
         sum_and_send(r + 1, False)
 

time: 48.2 us -> 47.6 us (0.988)
  Pallas kernels: 48 us -> 47.5 us
    pallas_call x1, Pallas kernels: 45.7 us -> 45.2 us  [on_device(): pl.pallas_call(functools.partial(kernel, seq_size), out_shape=(vmem((2 *...]
where the time goes in v5:
time: 47.6 us; the launch traced here: 47.5 us
  Pallas kernels  47.5 us (100%)
    pallas_call x1, Pallas kernels, on_device(): pl.pallas_call(functools.partial(kernel, seq_size), out_shape=(vmem((2 *...  45.2 us
    pallas_call x1, Pallas kernels, on_device(): pl.pallas_call(project, out_shape=jax.ShapeDtypeStruct((2 * K, columns),...  2.31 us

profile of v5, /device:TPU:97, one launch (start us, length us, event | category | flops | bytes accessed | tf_op | source)
XLA Modules:
  0.0 47.5 jit_solution(4200603460157953597)
XLA Ops:
  0.0 45.2 %shard_map.55 = (bf16[128,1280]{1,0:T(8,128)(2,1)S(1)}, bf16[8,1280,512]{2,1,0:T(8,128)(2,1)S(1)}) custom-call(s32[128]{0:T(128)} %starts.1, s32[64,128]{1,0:T(8,128)} %bitcast.1, f32[1280]{0:T(1024)} %gain.1, bf16[4096,1280]{1,0:T(8,128)(2,1)} %tok_hbm.1, bf16[1280,4096]{1,0:T(8,128)(2,1)} %w_hbm.1), custom_call_target="tpu_custom_call" | custom-call | tf_op jit(solution)/shard_map/pallas_call | solution.py:413
  45.2 2.3 %shard_map.56 = bf16[128,4096]{1,0:T(8,128)(2,1)} custom-call(bf16[128,1280]{1,0:T(8,128)(2,1)S(1)} %get-tuple-element.7.nm, bf16[8,1280,512]{2,1,0:T(8,128)(2,1)S(1)} %get-tuple-element.8.wp), custom_call_target="tpu_custom_call" | custom-call | tf_op jit(solution)/shard_map/pallas_call | solution.py:468
